TPU v7x, 32 devices: a whole 2x2x4 slice. The times are simulated.
32 devices in a mesh: rep: 32 (over z, y, x, core).
Axes of the slice: x: 2, y: 2, z: 4, core: 2. Of those that a mesh axis runs over, the one named last changes fastest.
Arguments:
- inputs: bfloat16 [16384, 1024], P('rep'), may hold values from -6 to 6
- out_grads: bfloat16 [16384, 4096], P('rep'), may hold values from -0.29882812 to 0.29882812
- error_in: bfloat16 [32, 1024, 4096], P('rep'), may hold values from -6 to 6
- q_start: float32 [32, 4096], replicated, may hold values from -0.09375 to 0.09375
- master: float32 [1024, 4096], P(None, 'rep'), may hold values from -1.2 to 1.2
Outputs:
- error_out: bfloat16 [32, 1024, 4096], P('rep')
- q_out: float32 [32, 4096], replicated
- master_out: float32 [1024, 4096], P(None, 'rep')
All inputs are finite; a program needn't handle non-finite values.
Results may differ from a plain program's by a relative error of at most 0.001.
Values sent between devices are 32-bit elements; how exact they have to be, the bound alone decides.
A program may use at most 128 MiB of HBM per device.

v0:
```python
import functools

import jax
import jax.numpy as jnp
from jax import lax
from jax.experimental import pallas as pl
from jax.experimental.pallas import tpu as pltpu
from jax.sharding import PartitionSpec as P

ITERS = 3
AXIS = "rep"
MESH = pl.DeviceIdType.MESH
F32, BF16 = jnp.float32, jnp.bfloat16


def split_tiles(count, rows, cols):
    col_cuts = min(count, cols // 128)
    row_cuts = max(1, min(count // col_cuts, rows // 8))
    return row_cuts, col_cuts, count // (row_cuts * col_cuts)


def halves(value):
    high = value.astype(BF16)
    return high, (value - high.astype(F32)).astype(BF16)


def kernel(
    count, x_hbm, dy_hbm, err_hbm, start_ref, master_ref,
    err_out, q_out, master_out,
    x_v, xt_v, dy_v, m_hi, m_lo,
    q_full, q_part, q_recv, q_split, p_full, p_part, p_recv, vecs, basis, b_split, b_tall, p_tall,
    load_sem, dy_sem, err_sem,
    p_rs_send, p_rs_recv, p_ag_send, p_ag_recv, q_rs_send, q_rs_recv, q_ag_send, q_ag_recv,
):
    me = lax.axis_index(AXIS)
    err_v = err_out.at[0]
    rank, width = p_full.shape
    ff = q_full.shape[1]
    step_cols = dy_sem.shape[0]
    cw = ff // step_cols

    pltpu.make_async_copy(x_hbm, x_v, load_sem).start()
    for c in range(step_cols):
        cols = pl.ds(c * cw, cw)
        pltpu.make_async_copy(dy_hbm.at[:, cols], dy_v.at[:, cols], dy_sem.at[c]).start()
        pltpu.make_async_copy(err_hbm.at[0, :, cols], err_v.at[:, cols], err_sem.at[c]).start()

    barrier = pltpu.get_barrier_semaphore()

    @pl.loop(1, count)
    def _(d):
        pl.semaphore_signal(barrier, inc=1, device_id=(lax.rem(me + d, count),), device_id_type=MESH)

    def piece(cuts, shape, owner):
        row_cuts, col_cuts, stride = cuts
        index = owner // stride
        rows, cols = shape[0] // row_cuts, shape[1] // col_cuts
        row = pl.multiple_of((index % row_cuts) * rows, rows)
        col = pl.multiple_of((index // row_cuts) * cols, cols)
        return pl.ds(row, rows), pl.ds(col, cols)

    def is_owner(cuts, device):
        return lax.rem(device, cuts[2]) == 0

    def guarded(cuts, device, body):
        if cuts[2] == 1:
            body()
        else:
            pl.when(is_owner(cuts, device))(body)

    def after(d):
        device = me + d
        return jnp.where(device < count, device, device - count)

    def drain(recv, sem, pieces):
        if pieces:
            ref = recv.at[pl.ds(0, pieces)]
            pltpu.make_async_copy(ref, ref, sem).wait()

    def either(cuts, owner_body, other_body):
        if cuts[2] == 1:
            owner_body()
        else:
            pl.when(is_owner(cuts, me))(owner_body)
            pl.when(jnp.logical_not(is_owner(cuts, me)))(other_body)

    def add_up(cuts, part, full, recv, recv_sem, ag_send, ag_recv, scale):
        def body():
            mine = piece(cuts, part.shape, me)
            drain(recv, recv_sem, count - 1)
            total = part[mine] + jnp.sum(recv[...], axis=0)
            full[mine] = total if scale == 1 else total / scale

            @pl.loop(1, count)
            def _(d):
                pltpu.make_async_remote_copy(
                    src_ref=full.at[mine], dst_ref=full.at[mine],
                    send_sem=ag_send, recv_sem=ag_recv,
                    device_id=(after(d),), device_id_type=MESH,
                ).start()

        either(cuts, body, lambda: None)

    def drain_sends(cuts, recv, rs_send, ag_send):
        owners = cuts[0] * cuts[1]

        def owner_body():
            drain(recv, rs_send, owners - 1)
            drain(recv, ag_send, count - 1)

        either(cuts, owner_body, lambda: drain(recv, rs_send, owners))

    p_cuts = split_tiles(count, rank, width)
    q_cuts = split_tiles(count, rank, ff)
    q_width = ff // q_cuts[1]
    members = cw // q_width * q_cuts[0]
    own_group = me // q_cuts[2] // members

    def columns(group):
        return pl.ds(pl.multiple_of(group * cw, cw), cw)

    def await_group(group):
        either(
            q_cuts,
            lambda: own_or_other(group),
            lambda: drain(q_recv, q_ag_recv.at[group], members),
        )

    def own_or_other(group):
        @pl.when(group == own_group)
        def _():
            drain(q_recv, q_ag_recv.at[group], members - 1)

        @pl.when(group != own_group)
        def _():
            drain(q_recv, q_ag_recv.at[group], members)

    def absorb(source, cols):
        high, low = halves(source[:, cols])
        factor = jnp.concatenate([high, low], axis=0)
        dims = (((1,), (1,)), ((), ()))
        tall = lax.dot_general(m_hi[:, cols], factor, dims, preferred_element_type=F32)
        tall += lax.dot_general(m_lo[:, cols], factor, dims, preferred_element_type=F32)
        p_tall[...] += tall

    def settle():
        flat = p_tall[...].T
        p_part[...] = flat[0:rank] + flat[rank:2 * rank]

        @pl.loop(1, count)
        def _(d):
            target = after(d)

            def send():
                pltpu.make_async_remote_copy(
                    src_ref=p_part.at[piece(p_cuts, p_part.shape, target)],
                    dst_ref=p_recv.at[d - 1],
                    send_sem=p_rs_send, recv_sem=p_rs_recv,
                    device_id=(target,), device_id_type=MESH,
                ).start()

            guarded(p_cuts, target, send)

        p_tall[...] = jnp.zeros_like(p_tall)

    pltpu.make_async_copy(x_hbm, x_v, load_sem).wait()
    xt_v[...] = x_v[...].T
    p_tall[...] = jnp.zeros_like(p_tall)

    @pl.loop(0, step_cols)
    def _(c):
        cols = pl.ds(pl.multiple_of(c * cw, cw), cw)
        pltpu.make_async_copy(dy_hbm.at[:, cols], dy_v.at[:, cols], dy_sem.at[c]).wait()
        pltpu.make_async_copy(err_hbm.at[0, :, cols], err_v.at[:, cols], err_sem.at[c]).wait()
        merged = jnp.dot(xt_v[...], dy_v[:, cols], preferred_element_type=F32)
        high, low = halves(merged + err_v[:, cols].astype(F32))
        m_hi[:, cols] = high
        m_lo[:, cols] = low
        absorb(start_ref, cols)

    pl.semaphore_wait(barrier, count - 1)
    settle()

    @pl.loop(0, ITERS)
    def _(step):
        add_up(p_cuts, p_part, p_full, p_recv, p_rs_recv, p_ag_send, p_ag_recv, 1)
        p_owners = p_cuts[0] * p_cuts[1]
        either(
            p_cuts,
            lambda: drain(p_recv, p_ag_recv, p_owners - 1),
            lambda: drain(p_recv, p_ag_recv, p_owners),
        )

        vecs[...] = p_full[...]
        for base in range(0, rank, 8):
            block = pl.ds(base, 8)
            above, rest = p_full[block, :], vecs[block, :]
            done = []
            for k in range(8):
                row = rest[k:k + 1, :]
                norm = jnp.sum(row * row, axis=1, keepdims=True) + 1.0
                coef = jnp.sum(above * row, axis=1, keepdims=True)
                inverse = lax.rsqrt(norm)
                unit = row * inverse
                done.append(unit)
                if k < 7:
                    rest = rest - (coef * inverse) * unit
                for below in range(base + 8, rank, 8):
                    later = pl.ds(below, 8)
                    coef = jnp.sum(p_full[later, :] * unit, axis=1, keepdims=True)
                    vecs[later, :] = vecs[later, :] - coef * unit
            basis[block, :] = jnp.concatenate(done, axis=0)

        high, low = halves(basis[...])
        b_split[0:rank] = high
        b_split[rank:2 * rank] = low

        groups = ff // cw

        @pl.loop(0, groups)
        def _(i):
            group = lax.rem(own_group + 1 + i, groups)
            cols = pl.ds(pl.multiple_of(group * cw, cw), cw)
            both = jnp.dot(b_split[...], m_hi[:, cols], preferred_element_type=F32)
            both += jnp.dot(b_split[...], m_lo[:, cols], preferred_element_type=F32)
            q_part[:, cols] = both[0:rank] + both[rank:2 * rank]

            for j in range(members):
                target = (group * members + j) * q_cuts[2]

                @pl.when(target != me)
                def _():
                    pltpu.make_async_remote_copy(
                        src_ref=q_part.at[piece(q_cuts, q_part.shape, target)],
                        dst_ref=q_recv.at[lax.rem(target - me + count, count) - 1],
                        send_sem=q_rs_send, recv_sem=q_rs_recv,
                        device_id=(target,), device_id_type=MESH,
                    ).start()

        add_up(
            q_cuts, q_part, q_full, q_recv, q_rs_recv, q_ag_send, q_ag_recv.at[own_group], count
        )

        drain_sends(p_cuts, p_recv, p_rs_send, p_ag_send)

        @pl.when(step < ITERS - 1)
        def _():
            @pl.loop(0, step_cols)
            def _(i):
                group = lax.rem(own_group - i + step_cols, step_cols)
                await_group(group)
                absorb(q_full, columns(group))

            settle()
            drain_sends(q_cuts, q_recv, q_rs_send, q_ag_send)

    tall = basis[...].T
    high, low = halves(tall)
    b_tall[:, 0:rank] = high
    b_tall[:, rank:2 * rank] = high
    b_tall[:, 2 * rank:3 * rank] = low

    @pl.loop(0, step_cols)
    def _(i):
        group = lax.rem(own_group - i + step_cols, step_cols)
        await_group(group)
        cols = columns(group)
        high, low = halves(q_full[:, cols])
        factor = jnp.concatenate([high, low, high], axis=0)
        q_split[:, cols] = factor
        recon = jnp.dot(b_tall[...], factor, preferred_element_type=F32)
        merged = m_hi[:, cols].astype(F32) + m_lo[:, cols].astype(F32)
        err_v[:, cols] = (merged - recon).astype(BF16)

    drain_sends(q_cuts, q_recv, q_rs_send, q_ag_send)
    q_out[...] = q_full[...]

    own = master_ref.shape[1]
    if own % 128 == 0:
        mine = q_split[:, pl.ds(pl.multiple_of(me * own, own), own)]
    else:
        base = pl.multiple_of((me * own) // 128 * 128, 128)
        block = q_split[:, pl.ds(base, 128)].astype(F32)
        shift = lax.rem(128 - lax.rem(me * own, 128), 128)
        mine = pltpu.roll(block, shift, 1)[:, 0:own].astype(BF16)
    master_out[...] = master_ref[...] - 0.5 * jnp.dot(b_tall[...], mine, preferred_element_type=F32)


def shards(inputs, out_grads, error_in, q_start, master):
    count = lax.axis_size(AXIS)
    tokens, width = inputs.shape
    ff = out_grads.shape[1]
    rank = q_start.shape[0]
    steps = ff // 512
    hbm_spec = pl.BlockSpec(memory_space=pltpu.HBM)
    vmem_spec = pl.BlockSpec(memory_space=pltpu.VMEM)
    p_cuts, q_cuts = split_tiles(count, rank, width), split_tiles(count, rank, ff)
    dma = pltpu.SemaphoreType.DMA
    return pl.pallas_call(
        functools.partial(kernel, count),
        out_shape=(
            pltpu.VMEM(error_in.shape, BF16),
            pltpu.VMEM(q_start.shape, F32),
            pltpu.VMEM(master.shape, F32),
        ),
        in_specs=[hbm_spec] * 3 + [vmem_spec] * 2,
        out_specs=(vmem_spec, vmem_spec, vmem_spec),
        scratch_shapes=[
            pltpu.VMEM((tokens, width), BF16),
            pltpu.VMEM((width, tokens), BF16),
            pltpu.VMEM((tokens, ff), BF16),
            pltpu.VMEM((width, ff), BF16),
            pltpu.VMEM((width, ff), BF16),
            pltpu.VMEM((rank, ff), F32),
            pltpu.VMEM((rank, ff), F32),
            pltpu.VMEM((count - 1, rank // q_cuts[0], ff // q_cuts[1]), F32),
            pltpu.VMEM((3 * rank, ff), BF16),
            pltpu.VMEM((rank, width), F32),
            pltpu.VMEM((rank, width), F32),
            pltpu.VMEM((count - 1, rank // p_cuts[0], width // p_cuts[1]), F32),
            pltpu.VMEM((rank, width), F32),
            pltpu.VMEM((rank, width), F32),
            pltpu.VMEM((2 * rank, width), BF16),
            pltpu.VMEM((width, 3 * rank), BF16),
            pltpu.VMEM((width, 2 * rank), F32),
            dma, dma((steps,)), dma((steps,)),
            dma, dma, dma, dma, dma, dma, dma, dma((steps,)),
        ],
        compiler_params=pltpu.CompilerParams(
            collective_id=0, has_side_effects=True, vmem_limit_bytes=44 * 1024 * 1024
        ),
    )(inputs, out_grads, error_in, q_start, master)


def solution(mesh):
    return jax.shard_map(
        shards,
        mesh=mesh,
        in_specs=(P("rep", None), P("rep", None), P("rep", None, None), P(), P(None, "rep")),
        out_specs=(P("rep", None, None), P(), P(None, "rep")),
        check_vma=False,
    )
```

profile of v0, /device:TPU:27, one launch (start us, length us, event | category | flops | bytes accessed | tf_op | source)
XLA Modules:
  0.0 161.7 jit_solution(9686584422494774823)
XLA Ops:
  0.6 0.0 copy-start
  0.6 1.0 copy-done
  1.7 155.0 %shard_map.76 = (bf16[1,1024,4096]{2,1,0:T(8,128)(2,1)S(1)}, f32[32,4096]{1,0:T(8,128)S(1)}, f32[1024,128]{1,0:T(8,128)S(1)}) custom-call(bf16[512,1024]{1,0:T(8,128)(2,1)} %x_hbm.1, bf16[512,4096]{1,0:T(8,128)(2,1)} %dy_hbm.1, bf16[1,1024,4096]{2,1,0:T(8,128)(2,1)} %err_hbm.1, f32[32,4096]{1,0:T(8,128)S(1)} %copy-done, f32[1024,128]{1,0:T(8,128)} %master_ref.1), custom_call_target="tpu_custom_call" | custom-call | tf_op jit(solution)/shard_map/pallas_call | solution.py:299
  156.7 3.4 %copy.11 = bf16[1,1024,4096]{2,1,0:T(8,128)(2,1)} copy(bf16[1,1024,4096]{2,1,0:T(8,128)(2,1)S(1)} %get-tuple-element.3) | data formatting | bytes 16777216
  160.1 0.8 copy.12
  160.9 0.8 copy.13
Async XLA Ops:
  0.6 1.0 copy-start
where the time goes:
time: 162 us
  Pallas kernels  155 us (96%)
  local copies, waits for them, and re-layouts  6.02 us (4%)
    pallas_call x1, Pallas kernels, shards(): pl.pallas_call(functools.partial(kernel, count), out_shape=(pltpu.VMEM(er...  155 us
    unnamed x5, local copies, waits for them, and re-layouts  6.02 us

commit v1 on v0

v1 whole, which is shorter than its diff:
```python
import functools

import jax
import jax.numpy as jnp
from jax import lax
from jax.experimental import pallas as pl
from jax.experimental.pallas import tpu as pltpu
from jax.sharding import PartitionSpec as P

ITERS = 3
AXIS = "rep"
CHUNK = 512
MESH = pl.DeviceIdType.MESH
F32, BF16 = jnp.float32, jnp.bfloat16


def split_tiles(count, rows, cols):
    col_cuts = min(count, cols // 128)
    row_cuts = max(1, min(count // col_cuts, rows // 8))
    return row_cuts, col_cuts, count // (row_cuts * col_cuts)


def split_columns(count, cols):
    col_cuts = min(count, cols // 128)
    return 1, col_cuts, count // col_cuts


def halves(value):
    high = value.astype(BF16)
    return high, (value - high.astype(F32)).astype(BF16)


def far_first(own, step, count):
    if count & (count - 1) == 0:
        return own ^ (count - step)
    return lax.rem(own + step, count)


def near_first(own, step, count):
    if count & (count - 1) == 0:
        return own ^ step
    return lax.rem(own - step + count, count)


def kernel(
    count, x_hbm, dy_hbm, err_hbm, start_hbm, master_hbm,
    err_out, q_out, master_out,
    x_v, xt_v, dy_v, merged, pair, m_hi, m_lo,
    q_full, q_part, q_recv, q_split, p_full, p_part, p_recv, vecs, basis, t_vecs, t_mat, b_split, b_tall, p_tall,
    load_sem, start_sem, master_sem, dy_sem, err_sem, pair_send, pair_recv, relay_send, relay_recv,
    p_rs_send, p_rs_recv, p_ag_send, p_ag_recv, q_rs_send, q_rs_recv, q_ag_send, q_ag_recv,
):
    me = lax.axis_index(AXIS)
    core, chip, chips = lax.rem(me, 2), me // 2, count // 2
    partner = me + 1 - 2 * core
    err_v = err_out.at[0]
    rank, width = p_full.shape
    ff = q_full.shape[1]
    half = ff // 2
    groups, _, cw = pair.shape
    own_base, other_base = core * half, (1 - core) * half

    def chunk(base, i):
        return pl.ds(pl.multiple_of(base + i * cw, cw), cw)

    def local(i):
        return pl.ds(pl.multiple_of(i * cw, cw), cw)

    own_half = pl.ds(pl.multiple_of(own_base, half), half)

    def chunk_loads(base, i, slot):
        cols = chunk(base, i)
        return (
            pltpu.make_async_copy(dy_hbm.at[:, cols], dy_v.at[:, cols], dy_sem.at[slot]),
            pltpu.make_async_copy(err_hbm.at[0, :, cols], err_v.at[:, cols], err_sem.at[slot]),
        )

    def start_loads(base, i, slot):
        for load in chunk_loads(base, i, slot):
            load.start()

    pltpu.make_async_copy(x_hbm, x_v, load_sem).start()
    start_loads(other_base, 0, 0)

    barrier = pltpu.get_barrier_semaphore()

    @pl.loop(1, count)
    def _(d):
        pl.semaphore_signal(barrier, inc=1, device_id=(lax.rem(me + d, count),), device_id_type=MESH)

    pltpu.make_async_copy(x_hbm, x_v, load_sem).wait()
    for i in range(1, groups):
        start_loads(other_base, i, i)
    for i in range(groups):
        start_loads(own_base, i, groups + i)
    start_load = pltpu.make_async_copy(start_hbm.at[:, own_half], q_full.at[:, own_half], start_sem)
    start_load.start()
    master_load = pltpu.make_async_copy(master_hbm, master_out, master_sem)
    master_load.start()
    xt_v[...] = x_v[...].T

    def piece(cuts, shape, owner):
        row_cuts, col_cuts, stride = cuts
        index = owner // stride
        rows, cols = shape[0] // row_cuts, shape[1] // col_cuts
        row = pl.multiple_of((index % row_cuts) * rows, rows)
        col = pl.multiple_of((index // row_cuts) * cols, cols)
        return row, rows, col, cols

    def window(cuts, shape, owner, shift=0):
        row, rows, col, cols = piece(cuts, shape, owner)
        return pl.ds(row, rows), pl.ds(pl.multiple_of(shift + col, cols), cols)

    def is_owner(cuts, place):
        return lax.rem(place, cuts[2]) == 0

    def guarded(cuts, place, body):
        if cuts[2] == 1:
            body()
        else:
            pl.when(is_owner(cuts, place))(body)

    def either(cuts, place, owner_body, other_body):
        if cuts[2] == 1:
            owner_body()
        else:
            pl.when(is_owner(cuts, place))(owner_body)
            pl.when(jnp.logical_not(is_owner(cuts, place)))(other_body)

    def drain(recv, sem, pieces):
        if pieces:
            ref = recv.at[pl.ds(0, pieces)]
            pltpu.make_async_copy(ref, ref, sem).wait()

    def drain_sends(cuts, place, peers, recv, rs_send, ag_send):
        owners = cuts[0] * cuts[1]

        def owner_body():
            drain(recv, rs_send, owners - 1)
            drain(recv, ag_send, peers - 1)

        either(cuts, place, owner_body, lambda: drain(recv, rs_send, owners))

    p_cuts = split_tiles(count, rank, width)
    q_cuts = split_columns(chips, half)
    p_owners, q_owners = p_cuts[0] * p_cuts[1], q_cuts[0] * q_cuts[1]
    members = cw // (half // q_cuts[1])
    own_group = chip // q_cuts[2] // members

    def absorb(group):
        high, low = halves(q_full[:, chunk(own_base, group)])
        factor = jnp.concatenate([high, low], axis=0)
        dims = (((1,), (1,)), ((), ()))
        cols = local(group)
        tall = lax.dot_general(m_hi[:, cols], factor, dims, preferred_element_type=F32)
        tall += lax.dot_general(m_lo[:, cols], factor, dims, preferred_element_type=F32)
        p_tall[...] += tall

    def settle():
        flat = p_tall[...].T
        p_part[...] = flat[0:rank] + flat[rank:2 * rank]

        @pl.loop(1, count)
        def _(d):
            target = far_first(me, d, count)

            def send():
                pltpu.make_async_remote_copy(
                    src_ref=p_part.at[window(p_cuts, p_part.shape, target)],
                    dst_ref=p_recv.at[lax.rem(target - me + count, count) - 1],
                    send_sem=p_rs_send, recv_sem=p_rs_recv,
                    device_id=(target,), device_id_type=MESH,
                ).start()

            guarded(p_cuts, target, send)

        p_tall[...] = jnp.zeros_like(p_tall)

    def merge(base, i, slot):
        cols = chunk(base, i)
        for load in chunk_loads(base, i, slot):
            load.wait()
        product = jnp.dot(xt_v[...], dy_v[:, cols], preferred_element_type=F32)
        merged[:, cols] = product + err_v[:, cols].astype(F32)
        return cols

    p_tall[...] = jnp.zeros_like(p_tall)
    pl.semaphore_wait(barrier, count - 1)

    @pl.loop(0, groups)
    def _(i):
        cols = merge(other_base, i, i)
        pltpu.make_async_remote_copy(
            src_ref=merged.at[:, cols], dst_ref=pair.at[i],
            send_sem=pair_send, recv_sem=pair_recv.at[i],
            device_id=(partner,), device_id_type=MESH,
        ).start()

    @pl.loop(0, groups)
    def _(i):
        merge(own_base, i, groups + i)

    start_load.wait()

    @pl.loop(0, groups)
    def _(i):
        pltpu.make_async_copy(pair.at[i], pair.at[i], pair_recv.at[i]).wait()
        high, low = halves(merged[:, chunk(own_base, i)] + pair[i])
        m_hi[:, local(i)] = high
        m_lo[:, local(i)] = low
        absorb(i)

    settle()
    pltpu.make_async_copy(pair, pair, pair_send).wait()

    def orthogonalize():
        vecs[...] = p_full[...]
        lanes = lax.broadcasted_iota(jnp.int32, t_vecs.shape, 1)
        t_vecs[...] = (lanes == lax.broadcasted_iota(jnp.int32, t_vecs.shape, 0)).astype(F32)
        for base in range(0, rank, 8):
            block = pl.ds(base, 8)
            above, rest, t_rest = p_full[block, :], vecs[block, :], t_vecs[block, :]
            done, t_done = [], []
            for k in range(8):
                row = rest[k:k + 1, :]
                norm = jnp.sum(row * row, axis=1, keepdims=True) + 1.0
                coef = jnp.sum(above * row, axis=1, keepdims=True)
                inverse = lax.rsqrt(norm)
                unit = row * inverse
                t_unit = t_rest[k:k + 1, :] * inverse
                done.append(unit)
                t_done.append(t_unit)
                if k < 7:
                    rest = rest - (coef * inverse) * unit
                    t_rest = t_rest - (coef * inverse) * t_unit
                for below in range(base + 8, rank, 8):
                    later = pl.ds(below, 8)
                    coef = jnp.sum(p_full[later, :] * unit, axis=1, keepdims=True)
                    vecs[later, :] = vecs[later, :] - coef * unit
                    t_vecs[later, :] = t_vecs[later, :] - coef * t_unit
            basis[block, :] = jnp.concatenate(done, axis=0)
            t_mat[block, :] = jnp.concatenate(t_done, axis=0)

    def sum_p():
        def body():
            mine = window(p_cuts, p_part.shape, me)
            drain(p_recv, p_rs_recv, count - 1)
            p_full[mine] = p_part[mine] + jnp.sum(p_recv[...], axis=0)

            @pl.loop(1, count)
            def _(d):
                pltpu.make_async_remote_copy(
                    src_ref=p_full.at[mine], dst_ref=p_full.at[mine],
                    send_sem=p_ag_send, recv_sem=p_ag_recv,
                    device_id=(far_first(me, d, count),), device_id_type=MESH,
                ).start()

        either(p_cuts, me, body, lambda: None)
        either(
            p_cuts, me,
            lambda: drain(p_recv, p_ag_recv, p_owners - 1),
            lambda: drain(p_recv, p_ag_recv, p_owners),
        )

    def sum_q():
        def body():
            drain(q_recv, q_rs_recv, chips - 1)
            total = q_part[window(q_cuts, q_part.shape, chip)] + jnp.sum(q_recv[...], axis=0)
            rotated = jnp.dot(
                t_mat[:, 0:rank], total, precision=lax.Precision.HIGHEST, preferred_element_type=F32
            )
            mine = window(q_cuts, q_part.shape, chip, own_base)
            q_full[mine] = rotated / count

            @pl.loop(1, chips)
            def _(d):
                pltpu.make_async_remote_copy(
                    src_ref=q_full.at[mine], dst_ref=q_full.at[mine],
                    send_sem=q_ag_send, recv_sem=q_ag_recv.at[own_group],
                    device_id=(2 * far_first(chip, d, chips) + core,), device_id_type=MESH,
                ).start()

        either(q_cuts, chip, body, lambda: None)

    def await_group(group):
        def own_or_other():
            @pl.when(group == own_group)
            def _():
                drain(q_recv, q_ag_recv.at[group], members - 1)

            @pl.when(group != own_group)
            def _():
                drain(q_recv, q_ag_recv.at[group], members)

        either(q_cuts, chip, own_or_other, lambda: drain(q_recv, q_ag_recv.at[group], members))

    @pl.loop(0, ITERS)
    def _(step):
        sum_p()
        high, low = halves(p_full[...])
        b_split[0:rank] = high
        b_split[rank:2 * rank] = low

        @pl.loop(0, groups)
        def _(i):
            group = far_first(own_group, i + 1, groups)
            cols = local(group)
            both = jnp.dot(b_split[...], m_hi[:, cols], preferred_element_type=F32)
            both += jnp.dot(b_split[...], m_lo[:, cols], preferred_element_type=F32)
            q_part[:, cols] = both[0:rank] + both[rank:2 * rank]

            for j in range(members):
                target = (group * members + j) * q_cuts[2]

                @pl.when(target != chip)
                def _():
                    pltpu.make_async_remote_copy(
                        src_ref=q_part.at[window(q_cuts, q_part.shape, target)],
                        dst_ref=q_recv.at[lax.rem(target - chip + chips, chips) - 1],
                        send_sem=q_rs_send, recv_sem=q_rs_recv,
                        device_id=(2 * target + core,), device_id_type=MESH,
                    ).start()

        orthogonalize()
        sum_q()
        drain_sends(p_cuts, me, count, p_recv, p_rs_send, p_ag_send)

        @pl.when(step < ITERS - 1)
        def _():
            @pl.loop(0, groups)
            def _(i):
                group = near_first(own_group, i, groups)
                await_group(group)
                absorb(group)

            settle()
            drain_sends(q_cuts, chip, chips, q_recv, q_rs_send, q_ag_send)

    tall = basis[...].T
    high, low = halves(tall)
    b_tall[:, 0:rank] = high
    b_tall[:, rank:2 * rank] = high
    b_tall[:, 2 * rank:3 * rank] = low

    def finish(cols):
        high, low = halves(q_full[:, cols])
        factor = jnp.concatenate([high, low, high], axis=0)
        q_split[:, cols] = factor
        recon = jnp.dot(b_tall[...], factor, preferred_element_type=F32)
        err_v[:, cols] = (merged[:, cols] - recon).astype(BF16)

    def relay(base, group):
        cols = chunk(base, group)
        return pltpu.make_async_remote_copy(
            src_ref=q_full.at[:, cols], dst_ref=q_full.at[:, cols],
            send_sem=relay_send, recv_sem=relay_recv.at[group],
            device_id=(partner,), device_id_type=MESH,
        )

    @pl.loop(0, groups)
    def _(i):
        group = near_first(own_group, i, groups)
        await_group(group)
        relay(own_base, group).start()
        finish(chunk(own_base, group))

    @pl.loop(0, groups)
    def _(i):
        group = near_first(own_group, i, groups)
        relay(other_base, group).wait_recv()
        finish(chunk(other_base, group))

    drain_sends(q_cuts, chip, chips, q_recv, q_rs_send, q_ag_send)
    pltpu.make_async_copy(q_part, q_part, relay_send).wait()
    q_out[...] = q_full[...]

    own = master_out.shape[1]
    if own % 128 == 0:
        mine = q_split[:, pl.ds(pl.multiple_of(me * own, own), own)]
    else:
        base = pl.multiple_of((me * own) // 128 * 128, 128)
        block = q_split[:, pl.ds(base, 128)].astype(F32)
        shift = lax.rem(128 - lax.rem(me * own, 128), 128)
        mine = pltpu.roll(block, shift, 1)[:, 0:own].astype(BF16)
    master_load.wait()
    master_out[...] = master_out[...] - 0.5 * jnp.dot(b_tall[...], mine, preferred_element_type=F32)


def shards(inputs, out_grads, error_in, q_start, master):
    count = lax.axis_size(AXIS)
    tokens, width = inputs.shape
    ff = out_grads.shape[1]
    rank = q_start.shape[0]
    chips, half = count // 2, ff // 2
    groups = half // CHUNK
    hbm_spec = pl.BlockSpec(memory_space=pltpu.HBM)
    vmem_spec = pl.BlockSpec(memory_space=pltpu.VMEM)
    p_cuts, q_cuts = split_tiles(count, rank, width), split_columns(chips, half)
    dma = pltpu.SemaphoreType.DMA
    return pl.pallas_call(
        functools.partial(kernel, count),
        out_shape=(
            pltpu.VMEM(error_in.shape, BF16),
            pltpu.VMEM(q_start.shape, F32),
            pltpu.VMEM(master.shape, F32),
        ),
        in_specs=[hbm_spec] * 5,
        out_specs=(vmem_spec, vmem_spec, vmem_spec),
        scratch_shapes=[
            pltpu.VMEM((tokens, width), BF16),
            pltpu.VMEM((width, tokens), BF16),
            pltpu.VMEM((tokens, ff), BF16),
            pltpu.VMEM((width, ff), F32),
            pltpu.VMEM((groups, width, CHUNK), F32),
            pltpu.VMEM((width, half), BF16),
            pltpu.VMEM((width, half), BF16),
            pltpu.VMEM((rank, ff), F32),
            pltpu.VMEM((rank, half), F32),
            pltpu.VMEM((chips - 1, rank // q_cuts[0], half // q_cuts[1]), F32),
            pltpu.VMEM((3 * rank, ff), BF16),
            pltpu.VMEM((rank, width), F32),
            pltpu.VMEM((rank, width), F32),
            pltpu.VMEM((count - 1, rank // p_cuts[0], width // p_cuts[1]), F32),
            pltpu.VMEM((rank, width), F32),
            pltpu.VMEM((rank, width), F32),
            pltpu.VMEM((rank, 128), F32),
            pltpu.VMEM((rank, 128), F32),
            pltpu.VMEM((2 * rank, width), BF16),
            pltpu.VMEM((width, 3 * rank), BF16),
            pltpu.VMEM((width, 2 * rank), F32),
            dma, dma, dma, dma((2 * groups,)), dma((2 * groups,)), dma, dma((groups,)), dma, dma((groups,)),
            dma, dma, dma, dma, dma, dma, dma, dma((groups,)),
        ],
        compiler_params=pltpu.CompilerParams(
            collective_id=0, has_side_effects=True, vmem_limit_bytes=52 * 1024 * 1024
        ),
    )(inputs, out_grads, error_in, q_start, master)


def solution(mesh):
    return jax.shard_map(
        shards,
        mesh=mesh,
        in_specs=(P("rep", None), P("rep", None), P("rep", None, None), P(), P(None, "rep")),
        out_specs=(P("rep", None, None), P(), P(None, "rep")),
        check_vma=False,
    )
```

time: 162 us -> 109 us (0.67)
  the two profiles are of different devices: /device:TPU:27 before, /device:TPU:0 now
where the time goes in v1:
time: 109 us
  Pallas kernels  104 us (95%)
  local copies, waits for them, and re-layouts  4.98 us (5%)
    pallas_call x1, Pallas kernels, shards(): pl.pallas_call(functools.partial(kernel, count), out_shape=(pltpu.VMEM(er...  104 us
    unnamed x3, local copies, waits for them, and re-layouts  4.98 us

profile of v1, /device:TPU:0, one launch (start us, length us, event | category | flops | bytes accessed | tf_op | source)
XLA Modules:
  0.0 109.2 jit_solution(6044588620419435309)
XLA Ops:
  0.6 103.6 %shard_map.76 = (bf16[1,1024,4096]{2,1,0:T(8,128)(2,1)S(1)}, f32[32,4096]{1,0:T(8,128)S(1)}, f32[1024,128]{1,0:T(8,128)S(1)}) custom-call(bf16[512,1024]{1,0:T(8,128)(2,1)} %x_hbm.1, bf16[512,4096]{1,0:T(8,128)(2,1)} %dy_hbm.1, bf16[1,1024,4096]{2,1,0:T(8,128)(2,1)} %err_hbm.1, f32[32,4096]{1,0:T(8,128)} %start_hbm.1, f32[1024,128]{1,0:T(8,128)} %master_hbm.1), custom_call_target="tpu_custom_call" | custom-call | tf_op jit(solution)/shard_map/pallas_call | solution.py:400
  104.2 3.4 %copy.11 = bf16[1,1024,4096]{2,1,0:T(8,128)(2,1)} copy(bf16[1,1024,4096]{2,1,0:T(8,128)(2,1)S(1)} %get-tuple-element.3) | data formatting | bytes 16777216
  107.6 0.8 copy.12
  108.4 0.8 copy.13

commit v2 on v1

v2 whole, which is shorter than its diff:
```python
import functools

import jax
import jax.numpy as jnp
from jax import lax
from jax.experimental import pallas as pl
from jax.experimental.pallas import tpu as pltpu
from jax.sharding import PartitionSpec as P

ITERS = 3
AXIS = "rep"
CHUNK = 512
EARLY, LATE = 2, 3
MESH = pl.DeviceIdType.MESH
F32, BF16 = jnp.float32, jnp.bfloat16


def split_tiles(count, rows, cols):
    col_cuts = min(count, cols // 128)
    row_cuts = max(1, min(count // col_cuts, rows // 8))
    return row_cuts, col_cuts, count // (row_cuts * col_cuts)


def split_columns(count, cols):
    col_cuts = min(count, cols // 128)
    return 1, col_cuts, count // col_cuts


def halves(value):
    high = value.astype(BF16)
    return high, (value - high.astype(F32)).astype(BF16)


def far_first(own, step, count):
    if count & (count - 1) == 0:
        return own ^ (count - step)
    return lax.rem(own + step, count)


def near_first(own, step, count):
    if count & (count - 1) == 0:
        return own ^ step
    return lax.rem(own - step + count, count)


def kernel(
    count, x_hbm, dy_hbm, err_hbm, start_hbm,
    err_own, rest, q_out, b_tall,
    x_v, xt_v, dy_v, err_v, merged, pair, m_hi, m_lo,
    q_full, q_part, q_recv, b_split, p_full, p_part, p_recv, vecs, basis, t_vecs, t_mat, p_tall, u_tall, p_flat,
    load_sem, start_sem, dy_sem, err_sem, pair_send, pair_recv, relay_send, relay_recv,
    p_rs_send, p_rs_recv, p_ag_send, p_ag_recv, q_rs_send, q_rs_recv, q_ag_send, q_ag_recv,
):
    me = lax.axis_index(AXIS)
    core, chip, chips = lax.rem(me, 2), me // 2, count // 2
    partner = me + 1 - 2 * core
    rank, width = p_full.shape
    ff = q_full.shape[1]
    half = ff // 2
    groups, _, cw = pair.shape
    own_base, other_base = core * half, (1 - core) * half

    def chunk(base, i):
        return pl.ds(pl.multiple_of(base + i * cw, cw), cw)

    def local(i):
        return pl.ds(pl.multiple_of(i * cw, cw), cw)

    def chunk_loads(base, i, slot):
        cols = chunk(base, i)
        return (
            pltpu.make_async_copy(dy_hbm.at[:, cols], dy_v.at[:, cols], dy_sem.at[slot]),
            pltpu.make_async_copy(err_hbm.at[0, :, cols], err_v.at[:, cols], err_sem.at[slot]),
        )

    def start_loads(base, i, slot):
        for load in chunk_loads(base, i, slot):
            load.start()

    pltpu.make_async_copy(x_hbm, x_v, load_sem).start()
    start_load = pltpu.make_async_copy(start_hbm, q_full, start_sem)
    start_load.start()
    start_loads(other_base, 0, 0)

    barrier = pltpu.get_barrier_semaphore()

    @pl.loop(1, count)
    def _(d):
        pl.semaphore_signal(barrier, inc=1, device_id=(lax.rem(me + d, count),), device_id_type=MESH)

    pltpu.make_async_copy(x_hbm, x_v, load_sem).wait()
    for i in range(1, groups):
        start_loads(other_base, i, i)
    for i in range(groups):
        start_loads(own_base, i, groups + i)
    xt_v[...] = x_v[...].T

    def owner_of(cuts, index):
        return index * cuts[2]

    def index_of(cuts, place):
        return place // cuts[2]

    def window(cuts, shape, index, shift=0):
        row_cuts, col_cuts = cuts[:2]
        rows, cols = shape[0] // row_cuts, shape[1] // col_cuts
        row = pl.multiple_of(lax.rem(index, row_cuts) * rows, rows)
        col = pl.multiple_of(shift + index // row_cuts * cols, cols)
        return pl.ds(row, rows), pl.ds(col, cols)

    def either(cuts, place, owner_body, other_body):
        if cuts[2] == 1:
            owner_body()
        else:
            owns = jnp.logical_and(lax.rem(place, cuts[2]) == 0, place < cuts[0] * cuts[1] * cuts[2])
            pl.when(owns)(owner_body)
            pl.when(jnp.logical_not(owns))(other_body)

    def drain(recv, sem, pieces):
        if pieces:
            ref = recv.at[pl.ds(0, pieces)]
            pltpu.make_async_copy(ref, ref, sem).wait()

    def drain_sends(cuts, place, peers, recv, rs_send, ag_send):
        owners = cuts[0] * cuts[1]

        def owner_body():
            drain(recv, rs_send, owners - 1)
            drain(recv, ag_send, peers - 1)

        either(cuts, place, owner_body, lambda: drain(recv, rs_send, owners))

    p_cuts = split_tiles(count, rank, width)
    q_cuts = split_columns(chips, half)
    p_owners, q_owners = p_cuts[0] * p_cuts[1], q_cuts[0] * q_cuts[1]
    members = cw // (half // q_cuts[1])
    own_group = jnp.minimum(index_of(q_cuts, chip), q_owners - 1) // members

    def split_factor(cols):
        high, low = halves(q_full[:, cols])
        return jnp.concatenate([high, low], axis=0)

    def tall_dot(left, factor):
        return lax.dot_general(left, factor, (((1,), (1,)), ((), ())), preferred_element_type=F32)

    block = max(256, width // p_cuts[1])
    blocks = width // block
    sharers = p_cuts[0] * (block // (width // p_cuts[1]))
    own_block = jnp.minimum(index_of(p_cuts, me), p_owners - 1) // sharers

    def block_of(index):
        return pl.ds(pl.multiple_of(index * block, block), block)

    def send_block(index):
        for j in range(sharers):
            place = index * sharers + j
            target = owner_of(p_cuts, place)

            @pl.when(target != me)
            def _():
                pltpu.make_async_remote_copy(
                    src_ref=p_part.at[window(p_cuts, p_part.shape, place)],
                    dst_ref=p_recv.at[lax.rem(target - me + count, count) - 1],
                    send_sem=p_rs_send, recv_sem=p_rs_recv,
                    device_id=(target,), device_id_type=MESH,
                ).start()

    def absorb(group):
        factor = split_factor(chunk(own_base, group))
        cols = local(group)
        p_flat[...] += tall_dot(factor, m_hi[:, cols]) + tall_dot(factor, m_lo[:, cols])

    def absorb_last(group):
        factor = split_factor(chunk(own_base, group))
        cols = local(group)

        @pl.loop(0, blocks)
        def _(i):
            index = far_first(own_block, i + 1, blocks)
            rows = block_of(index)
            flat = p_flat[:, rows] + tall_dot(factor, m_hi[rows, cols]) + tall_dot(factor, m_lo[rows, cols])
            p_part[:, rows] = flat[0:rank] + flat[rank:2 * rank]
            send_block(index)

        p_flat[...] = jnp.zeros_like(p_flat)

    def merge(base, i, into):
        cols = chunk(base, i)
        product = jnp.dot(xt_v[...], dy_v[:, cols], preferred_element_type=F32)
        into[:, local(i)] = product + err_v[:, cols].astype(F32)

    def await_loads(base, i, slot):
        for load in chunk_loads(base, i, slot):
            load.wait()

    def first_factor(base, i):
        cols = chunk(base, i)
        factor = split_factor(cols)
        p_tall[...] += tall_dot(err_v[:, cols], factor)
        u_tall[...] += tall_dot(dy_v[:, cols], factor)

    def send_pair(i):
        pltpu.make_async_remote_copy(
            src_ref=rest.at[:, local(i)], dst_ref=pair.at[i],
            send_sem=pair_send, recv_sem=pair_recv.at[i],
            device_id=(partner,), device_id_type=MESH,
        ).start()

    p_tall[...] = jnp.zeros_like(p_tall)
    u_tall[...] = jnp.zeros_like(u_tall)
    pl.semaphore_wait(barrier, count - 1)
    start_load.wait()

    @pl.loop(0, groups)
    def _(i):
        await_loads(other_base, i, i)
        first_factor(other_base, i)

        @pl.when(i < EARLY)
        def _():
            merge(other_base, i, rest)
            send_pair(i)

    @pl.loop(0, groups)
    def _(i):
        await_loads(own_base, i, groups + i)
        first_factor(own_base, i)

    u_flat = u_tall[...].T
    high, low = halves(u_flat[0:rank] + u_flat[rank:2 * rank])
    u_split = jnp.concatenate([high, low], axis=0)

    @pl.loop(0, blocks)
    def _(i):
        index = far_first(own_block, i + 1, blocks)
        cols = block_of(index)
        flat = p_tall[cols, :].T + jnp.dot(u_split, x_v[:, cols], preferred_element_type=F32)
        p_part[:, cols] = flat[0:rank] + flat[rank:2 * rank]
        send_block(index)

    p_flat[...] = jnp.zeros_like(p_flat)

    @pl.loop(EARLY, groups)
    def _(i):
        merge(other_base, i, rest)
        pl.when(i < LATE)(lambda: send_pair(i))

    @pl.loop(0, groups // 2)
    def _(i):
        merge(own_base, i, merged)

    def add_pair():
        for i in range(LATE, groups):
            send_pair(i)

        @pl.loop(groups // 2, groups)
        def _(i):
            merge(own_base, i, merged)

        @pl.loop(0, groups)
        def _(i):
            pltpu.make_async_copy(pair.at[i], pair.at[i], pair_recv.at[i]).wait()
            high, low = halves(merged[:, local(i)] + pair[i])
            m_hi[:, local(i)] = high
            m_lo[:, local(i)] = low

        pltpu.make_async_copy(pair, pair, pair_send).wait()

    def orthogonalize():
        vecs[...] = p_full[...]
        lanes = lax.broadcasted_iota(jnp.int32, t_vecs.shape, 1)
        t_vecs[...] = (lanes == lax.broadcasted_iota(jnp.int32, t_vecs.shape, 0)).astype(F32)
        for base in range(0, rank, 8):
            band = pl.ds(base, 8)
            above, left, t_left = p_full[band, :], vecs[band, :], t_vecs[band, :]
            done, t_done = [], []
            for k in range(8):
                row = left[k:k + 1, :]
                norm = jnp.sum(row * row, axis=1, keepdims=True) + 1.0
                coef = jnp.sum(above * row, axis=1, keepdims=True)
                inverse = lax.rsqrt(norm)
                unit = row * inverse
                t_unit = t_left[k:k + 1, :] * inverse
                done.append(unit)
                t_done.append(t_unit)
                if k < 7:
                    left = left - (coef * inverse) * unit
                    t_left = t_left - (coef * inverse) * t_unit
                for below in range(base + 8, rank, 8):
                    later = pl.ds(below, 8)
                    coef = jnp.sum(p_full[later, :] * unit, axis=1, keepdims=True)
                    vecs[later, :] = vecs[later, :] - coef * unit
                    t_vecs[later, :] = t_vecs[later, :] - coef * t_unit
            basis[band, :] = jnp.concatenate(done, axis=0)
            t_mat[band, :] = jnp.concatenate(t_done, axis=0)

    def sum_p():
        def body():
            mine = window(p_cuts, p_part.shape, index_of(p_cuts, me))
            drain(p_recv, p_rs_recv, count - 1)
            p_full[mine] = p_part[mine] + jnp.sum(p_recv[...], axis=0)

            @pl.loop(1, count)
            def _(d):
                pltpu.make_async_remote_copy(
                    src_ref=p_full.at[mine], dst_ref=p_full.at[mine],
                    send_sem=p_ag_send, recv_sem=p_ag_recv.at[own_block],
                    device_id=(far_first(me, d, count),), device_id_type=MESH,
                ).start()

        either(p_cuts, me, body, lambda: None)

    def await_block(index):
        def own_or_other():
            @pl.when(index == own_block)
            def _():
                drain(p_recv, p_ag_recv.at[index], sharers - 1)

            @pl.when(index != own_block)
            def _():
                drain(p_recv, p_ag_recv.at[index], sharers)

        either(p_cuts, me, own_or_other, lambda: drain(p_recv, p_ag_recv.at[index], sharers))

    def send_group(group):
        for j in range(members):
            place = group * members + j
            target = owner_of(q_cuts, place)

            @pl.when(target != chip)
            def _():
                pltpu.make_async_remote_copy(
                    src_ref=q_part.at[window(q_cuts, q_part.shape, place)],
                    dst_ref=q_recv.at[lax.rem(target - chip + chips, chips) - 1],
                    send_sem=q_rs_send, recv_sem=q_rs_recv,
                    device_id=(2 * target + core,), device_id_type=MESH,
                ).start()

    def multiply():
        @pl.loop(0, blocks)
        def _(i):
            await_block(near_first(own_block, i, blocks))

        high, low = halves(p_full[...])
        left = jnp.concatenate([high, low], axis=0)
        b_split[...] = left

        @pl.loop(0, groups)
        def _(i):
            group = far_first(own_group, i + 1, groups)
            cols = local(group)
            both = jnp.dot(b_split[...], m_hi[:, cols], preferred_element_type=F32)
            both += jnp.dot(b_split[...], m_lo[:, cols], preferred_element_type=F32)
            q_part[:, cols] = both[0:rank] + both[rank:2 * rank]
            send_group(group)

    def sum_q():
        def body():
            drain(q_recv, q_rs_recv, chips - 1)
            index = index_of(q_cuts, chip)
            total = q_part[window(q_cuts, q_part.shape, index)] + jnp.sum(q_recv[...], axis=0)
            rotated = jnp.dot(
                t_mat[:, 0:rank], total, precision=lax.Precision.HIGHEST, preferred_element_type=F32
            )
            mine = window(q_cuts, q_part.shape, index, own_base)
            q_full[mine] = rotated / count

            @pl.loop(1, chips)
            def _(d):
                pltpu.make_async_remote_copy(
                    src_ref=q_full.at[mine], dst_ref=q_full.at[mine],
                    send_sem=q_ag_send, recv_sem=q_ag_recv.at[own_group],
                    device_id=(2 * far_first(chip, d, chips) + core,), device_id_type=MESH,
                ).start()

        either(q_cuts, chip, body, lambda: None)

    def await_group(group):
        def own_or_other():
            @pl.when(group == own_group)
            def _():
                drain(q_recv, q_ag_recv.at[group], members - 1)

            @pl.when(group != own_group)
            def _():
                drain(q_recv, q_ag_recv.at[group], members)

        either(q_cuts, chip, own_or_other, lambda: drain(q_recv, q_ag_recv.at[group], members))

    @pl.loop(0, ITERS)
    def _(step):
        sum_p()
        pl.when(step == 0)(add_pair)
        multiply()
        orthogonalize()
        sum_q()
        drain_sends(p_cuts, me, count, p_recv, p_rs_send, p_ag_send)

        @pl.when(step < ITERS - 1)
        def _():
            @pl.loop(0, groups - 1)
            def _(i):
                group = near_first(own_group, i, groups)
                await_group(group)
                absorb(group)

            group = near_first(own_group, groups - 1, groups)
            await_group(group)
            absorb_last(group)
            drain_sends(q_cuts, chip, chips, q_recv, q_rs_send, q_ag_send)

    tall = basis[...].T
    high, low = halves(tall)
    b_tall[:, 0:rank] = high
    b_tall[:, rank:2 * rank] = high
    b_tall[:, 2 * rank:3 * rank] = low

    def relay(base, group):
        cols = chunk(base, group)
        return pltpu.make_async_remote_copy(
            src_ref=q_full.at[:, cols], dst_ref=q_full.at[:, cols],
            send_sem=relay_send, recv_sem=relay_recv.at[group],
            device_id=(partner,), device_id_type=MESH,
        )

    @pl.loop(0, groups)
    def _(i):
        group = near_first(own_group, i, groups)
        await_group(group)
        relay(own_base, group).start()
        cols = local(group)
        err_own[:, cols] = (merged[:, cols] - recon(b_tall, q_full, chunk(own_base, group))).astype(BF16)

    @pl.loop(0, groups)
    def _(i):
        relay(other_base, i).wait_recv()

    drain_sends(q_cuts, chip, chips, q_recv, q_rs_send, q_ag_send)
    pltpu.make_async_copy(q_part, q_part, relay_send).wait()
    q_out[...] = q_full[...]


def recon(b_tall, q_full, cols):
    high, low = halves(q_full[:, cols])
    factor = jnp.concatenate([high, low, high], axis=0)
    return jnp.dot(b_tall[...], factor, preferred_element_type=F32)


def finish(
    err_own, rest, q_full, b_tall, master_hbm, err_out, q_out, master_out, tiles, master_v, load_sem, send_sem
):
    me = lax.axis_index(AXIS)
    core = lax.rem(me, 2)
    groups, _, cw = tiles.shape
    half = groups * cw
    own_base, other_base = core * half, (1 - core) * half
    load = pltpu.make_async_copy(master_hbm, master_v, load_sem)
    load.start()
    own_store = pltpu.make_async_copy(
        err_own, err_out.at[0, :, pl.ds(pl.multiple_of(own_base, half), half)], send_sem.at[groups]
    )
    own_store.start()
    q_store = pltpu.make_async_copy(q_full, q_out, send_sem.at[groups + 1])
    q_store.start()

    def store(i):
        cols = pl.ds(pl.multiple_of(other_base + i * cw, cw), cw)
        return pltpu.make_async_copy(tiles.at[i], err_out.at[0, :, cols], send_sem.at[i])

    @pl.loop(0, groups)
    def _(i):
        cols = pl.ds(pl.multiple_of(other_base + i * cw, cw), cw)
        local = pl.ds(pl.multiple_of(i * cw, cw), cw)
        tiles[i] = (rest[:, local] - recon(b_tall, q_full, cols)).astype(BF16)
        store(i).start()

    own = master_v.shape[1]
    span = max(own, 128)
    base = pl.multiple_of((me * own) // span * span, span)
    change = recon(b_tall, q_full, pl.ds(base, span))
    if own < span:
        change = pltpu.roll(change, lax.rem(span - lax.rem(me * own, span), span), 1)[:, 0:own]
    load.wait()
    master_v[...] = master_v[...] - 0.5 * change
    master_store = pltpu.make_async_copy(master_v, master_out, send_sem.at[groups + 2])
    master_store.start()

    @pl.loop(0, groups)
    def _(i):
        store(i).wait()

    own_store.wait()
    q_store.wait()
    master_store.wait()


def shards(inputs, out_grads, error_in, q_start, master):
    count = lax.axis_size(AXIS)
    tokens, width = inputs.shape
    ff = out_grads.shape[1]
    rank = q_start.shape[0]
    chips, half = count // 2, ff // 2
    groups = half // CHUNK
    hbm_spec = pl.BlockSpec(memory_space=pltpu.HBM)
    vmem_spec = pl.BlockSpec(memory_space=pltpu.VMEM)
    p_cuts, q_cuts = split_tiles(count, rank, width), split_columns(chips, half)
    blocks = width // max(256, width // p_cuts[1])
    dma = pltpu.SemaphoreType.DMA
    parts = pl.pallas_call(
        functools.partial(kernel, count),
        out_shape=(
            pltpu.VMEM((width, half), BF16),
            pltpu.VMEM((width, half), F32),
            pltpu.VMEM((rank, ff), F32),
            pltpu.VMEM((width, 3 * rank), BF16),
        ),
        in_specs=[hbm_spec] * 4,
        out_specs=(vmem_spec,) * 4,
        scratch_shapes=[
            pltpu.VMEM((tokens, width), BF16),
            pltpu.VMEM((width, tokens), BF16),
            pltpu.VMEM((tokens, ff), BF16),
            pltpu.VMEM((width, ff), BF16),
            pltpu.VMEM((width, half), F32),
            pltpu.VMEM((groups, width, CHUNK), F32),
            pltpu.VMEM((width, half), BF16),
            pltpu.VMEM((width, half), BF16),
            pltpu.VMEM((rank, ff), F32),
            pltpu.VMEM((rank, half), F32),
            pltpu.VMEM((chips - 1, rank // q_cuts[0], half // q_cuts[1]), F32),
            pltpu.VMEM((2 * rank, width), BF16),
            pltpu.VMEM((rank, width), F32),
            pltpu.VMEM((rank, width), F32),
            pltpu.VMEM((count - 1, rank // p_cuts[0], width // p_cuts[1]), F32),
            pltpu.VMEM((rank, width), F32),
            pltpu.VMEM((rank, width), F32),
            pltpu.VMEM((rank, 128), F32),
            pltpu.VMEM((rank, 128), F32),
            pltpu.VMEM((width, 2 * rank), F32),
            pltpu.VMEM((tokens, 2 * rank), F32),
            pltpu.VMEM((2 * rank, width), F32),
            dma, dma, dma((2 * groups,)), dma((2 * groups,)), dma, dma((groups,)), dma, dma((groups,)),
            dma, dma, dma, dma((blocks,)), dma, dma, dma, dma((groups,)),
        ],
        compiler_params=pltpu.CompilerParams(
            collective_id=0, has_side_effects=True, vmem_limit_bytes=47 * 1024 * 1024
        ),
    )(inputs, out_grads, error_in, q_start)
    return pl.pallas_call(
        finish,
        out_shape=(
            jax.ShapeDtypeStruct(error_in.shape, BF16),
            jax.ShapeDtypeStruct(q_start.shape, F32),
            jax.ShapeDtypeStruct(master.shape, F32),
        ),
        in_specs=[vmem_spec] * 4 + [hbm_spec],
        out_specs=(hbm_spec,) * 3,
        scratch_shapes=[
            pltpu.VMEM((groups, width, CHUNK), BF16),
            pltpu.VMEM(master.shape, F32),
            dma, dma((groups + 3,)),
        ],
        compiler_params=pltpu.CompilerParams(vmem_limit_bytes=16 * 1024 * 1024),
    )(*parts, master)


def solution(mesh):
    return jax.shard_map(
        shards,
        mesh=mesh,
        in_specs=(P("rep", None), P("rep", None), P("rep", None, None), P(), P(None, "rep")),
        out_specs=(P("rep", None, None), P(), P(None, "rep")),
        check_vma=False,
    )
```

time: 109 us -> 98.5 us (0.904)
  Pallas kernels: 104 us -> 97.7 us
  local copies, waits for them, and re-layouts: 4.98 us -> 0.01 us
    pallas_call x1 -> x2, Pallas kernels: 104 us -> 97.7 us  [the longest x1 94 us: shards(): pl.pallas_call(functools.partial(kernel, count), out_shape=(pltpu.VMEM((w...]
    unnamed x3 -> x2, local copies, waits for them, and re-layouts: 4.98 us -> 0.01 us
where the time goes in v2:
time: 98.5 us; the launch traced here: 98.4 us
  Pallas kernels  97.7 us (99%)
    pallas_call x1, Pallas kernels, shards(): pl.pallas_call(functools.partial(kernel, count), out_shape=(pltpu.VMEM((w...  94 us
    pallas_call x1, Pallas kernels, shards(): pl.pallas_call(finish, out_shape=(jax.ShapeDtypeStruct(error_in.shape, BF...  3.71 us

profile of v2, /device:TPU:0, one launch (start us, length us, event | category | flops | bytes accessed | tf_op | source)
XLA Modules:
  0.0 98.4 jit_solution(5836941457181703211)
XLA Ops:
  0.6 0.0 copy-start
  0.6 94.0 %shard_map.76 = (bf16[1024,2048]{1,0:T(8,128)(2,1)S(1)}, f32[1024,2048]{1,0:T(8,128)S(1)}, f32[32,4096]{1,0:T(8,128)S(1)}, bf16[1024,96]{1,0:T(8,128)(2,1)S(1)}) custom-call(bf16[512,1024]{1,0:T(8,128)(2,1)} %x_hbm.1, bf16[512,4096]{1,0:T(8,128)(2,1)} %dy_hbm.1, bf16[1,1024,4096]{2,1,0:T(8,128)(2,1)} %err_hbm.1, f32[32,4096]{1,0:T(8,128)} %start_hbm.1), custom_call_target="tpu_custom_call" | custom-call | tf_op jit(solution)/shard_map/pallas_call | solution.py:509
  94.6 0.0 copy-done
  94.6 3.7 %shard_map.77 = (bf16[1,1024,4096]{2,1,0:T(8,128)(2,1)}, f32[32,4096]{1,0:T(8,128)}, f32[1024,128]{1,0:T(8,128)}) custom-call(bf16[1024,2048]{1,0:T(8,128)(2,1)S(1)} %get-tuple-element.7.err_own, f32[1024,2048]{1,0:T(8,128)S(1)} %get-tuple-element.8.rest, f32[32,4096]{1,0:T(8,128)S(1)} %get-tuple-element.9.q_full, ...), custom_call_target="tpu_custom_call" | custom-call | tf_op jit(solution)/shard_map/pallas_call | solution.py:549
Async XLA Ops:
  0.6 94.0 %copy-start = (f32[1024,128]{1,0:T(8,128)S(1)}, f32[1024,128]{1,0:T(8,128)}, u32[]{:S(2)}) copy-start(f32[1024,128]{1,0:T(8,128)} %master_hbm.1) | copy-start | bytes 1572868

commit v3 on v2

--- a/solution.py
+++ b/solution.py
@@ -8,6 +8,8 @@
 from jax.sharding import PartitionSpec as P
 
 ITERS = 3
+STREAMS = 2
+MIDDLE = True
 AXIS = "rep"
 CHUNK = 512
 EARLY, LATE = 2, 3
@@ -16,14 +18,15 @@
 
 
 def split_tiles(count, rows, cols):
-    col_cuts = min(count, cols // 128)
-    row_cuts = max(1, min(count // col_cuts, rows // 8))
-    return row_cuts, col_cuts, count // (row_cuts * col_cuts)
+    pool, first = (count // 2, count // 4) if MIDDLE and count % 4 == 0 else (count, 0)
+    col_cuts = min(pool, cols // 128)
+    row_cuts = max(1, min(pool // col_cuts, rows // 8))
+    return row_cuts, col_cuts, pool // (row_cuts * col_cuts), first
 
 
 def split_columns(count, cols):
     col_cuts = min(count, cols // 128)
-    return 1, col_cuts, count // col_cuts
+    return 1, col_cuts, count // col_cuts, 0
 
 
 def halves(value):
@@ -47,7 +50,7 @@
     count, x_hbm, dy_hbm, err_hbm, start_hbm,
     err_own, rest, q_out, b_tall,
     x_v, xt_v, dy_v, err_v, merged, pair, m_hi, m_lo,
-    q_full, q_part, q_recv, b_split, p_full, p_part, p_recv, vecs, basis, t_vecs, t_mat, p_tall, u_tall, p_flat,
+    q_full, q_part, q_recv, q_sum, p_full, p_part, p_recv, vecs, basis, t_vecs, t_mat, p_tall, u_tall, p_flat,
     load_sem, start_sem, dy_sem, err_sem, pair_send, pair_recv, relay_send, relay_recv,
     p_rs_send, p_rs_recv, p_ag_send, p_ag_recv, q_rs_send, q_rs_recv, q_ag_send, q_ag_recv,
 ):
@@ -55,6 +58,7 @@
     core, chip, chips = lax.rem(me, 2), me // 2, count // 2
     partner = me + 1 - 2 * core
     rank, width = p_full.shape
+    band = rank // STREAMS
     ff = q_full.shape[1]
     half = ff // 2
     groups, _, cw = pair.shape
@@ -95,24 +99,29 @@
         start_loads(own_base, i, groups + i)
     xt_v[...] = x_v[...].T
 
+    def rows_of(h):
+        return pl.ds(h * band, band)
+
     def owner_of(cuts, index):
-        return index * cuts[2]
+        return cuts[3] + index * cuts[2]
 
     def index_of(cuts, place):
-        return place // cuts[2]
-
-    def window(cuts, shape, index, shift=0):
+        return jnp.clip((place - cuts[3]) // cuts[2], 0, cuts[0] * cuts[1] - 1)
+
+    def window(cuts, cols, index, h, shift=0):
         row_cuts, col_cuts = cuts[:2]
-        rows, cols = shape[0] // row_cuts, shape[1] // col_cuts
-        row = pl.multiple_of(lax.rem(index, row_cuts) * rows, rows)
+        rows, cols = band // row_cuts, cols // col_cuts
+        row = pl.multiple_of(h * band + lax.rem(index, row_cuts) * rows, rows)
         col = pl.multiple_of(shift + index // row_cuts * cols, cols)
         return pl.ds(row, rows), pl.ds(col, cols)
 
-    def either(cuts, place, owner_body, other_body):
-        if cuts[2] == 1:
+    def either(cuts, place, peers, owner_body, other_body):
+        row_cuts, col_cuts, stride, first = cuts
+        if row_cuts * col_cuts == peers:
             owner_body()
         else:
-            owns = jnp.logical_and(lax.rem(place, cuts[2]) == 0, place < cuts[0] * cuts[1] * cuts[2])
+            inside = jnp.logical_and(place >= first, place < first + row_cuts * col_cuts * stride)
+            owns = jnp.logical_and(inside, lax.rem(place - first + stride * peers, stride) == 0)
             pl.when(owns)(owner_body)
             pl.when(jnp.logical_not(owns))(other_body)
 
@@ -128,13 +137,13 @@
             drain(recv, rs_send, owners - 1)
             drain(recv, ag_send, peers - 1)
 
-        either(cuts, place, owner_body, lambda: drain(recv, rs_send, owners))
-
-    p_cuts = split_tiles(count, rank, width)
+        either(cuts, place, peers, owner_body, lambda: drain(recv, rs_send, owners))
+
+    p_cuts = split_tiles(count, band, width)
     q_cuts = split_columns(chips, half)
     p_owners, q_owners = p_cuts[0] * p_cuts[1], q_cuts[0] * q_cuts[1]
     members = cw // (half // q_cuts[1])
-    own_group = jnp.minimum(index_of(q_cuts, chip), q_owners - 1) // members
+    own_group = index_of(q_cuts, chip) // members
 
     def split_factor(cols):
         high, low = halves(q_full[:, cols])
@@ -146,12 +155,12 @@
     block = max(256, width // p_cuts[1])
     blocks = width // block
     sharers = p_cuts[0] * (block // (width // p_cuts[1]))
-    own_block = jnp.minimum(index_of(p_cuts, me), p_owners - 1) // sharers
+    own_block = index_of(p_cuts, me) // sharers
 
     def block_of(index):
         return pl.ds(pl.multiple_of(index * block, block), block)
 
-    def send_block(index):
+    def send_block(h, index):
         for j in range(sharers):
             place = index * sharers + j
             target = owner_of(p_cuts, place)
@@ -159,30 +168,34 @@
             @pl.when(target != me)
             def _():
                 pltpu.make_async_remote_copy(
-                    src_ref=p_part.at[window(p_cuts, p_part.shape, place)],
-                    dst_ref=p_recv.at[lax.rem(target - me + count, count) - 1],
-                    send_sem=p_rs_send, recv_sem=p_rs_recv,
+                    src_ref=p_part.at[window(p_cuts, width, place, h)],
+                    dst_ref=p_recv.at[h, lax.rem(target - me + count, count) - 1],
+                    send_sem=p_rs_send.at[h], recv_sem=p_rs_recv.at[h],
                     device_id=(target,), device_id_type=MESH,
                 ).start()
 
-    def absorb(group):
-        factor = split_factor(chunk(own_base, group))
+    def band_factor(h, group):
+        high, low = halves(q_full[rows_of(h), chunk(own_base, group)])
+        return jnp.concatenate([high, low], axis=0)
+
+    def absorb(h, group):
+        factor = band_factor(h, group)
         cols = local(group)
-        p_flat[...] += tall_dot(factor, m_hi[:, cols]) + tall_dot(factor, m_lo[:, cols])
-
-    def absorb_last(group):
-        factor = split_factor(chunk(own_base, group))
+        p_flat[h] += tall_dot(factor, m_hi[:, cols]) + tall_dot(factor, m_lo[:, cols])
+
+    def absorb_last(h, group):
+        factor = band_factor(h, group)
         cols = local(group)
 
         @pl.loop(0, blocks)
         def _(i):
             index = far_first(own_block, i + 1, blocks)
             rows = block_of(index)
-            flat = p_flat[:, rows] + tall_dot(factor, m_hi[rows, cols]) + tall_dot(factor, m_lo[rows, cols])
-            p_part[:, rows] = flat[0:rank] + flat[rank:2 * rank]
-            send_block(index)
-
-        p_flat[...] = jnp.zeros_like(p_flat)
+            flat = p_flat[h, :, rows] + tall_dot(factor, m_hi[rows, cols]) + tall_dot(factor, m_lo[rows, cols])
+            p_part[rows_of(h), rows] = flat[0:band] + flat[band:2 * band]
+            send_block(h, index)
+
+        p_flat[h] = jnp.zeros_like(p_flat[h])
 
     def merge(base, i, into):
         cols = chunk(base, i)
@@ -236,7 +249,13 @@
         cols = block_of(index)
         flat = p_tall[cols, :].T + jnp.dot(u_split, x_v[:, cols], preferred_element_type=F32)
         p_part[:, cols] = flat[0:rank] + flat[rank:2 * rank]
-        send_block(index)
+        send_block(0, index)
+
+    for h in range(1, STREAMS):
+
+        @pl.loop(0, blocks)
+        def _(i):
+            send_block(h, far_first(own_block, i + 1, blocks))
 
     p_flat[...] = jnp.zeros_like(p_flat)
 
@@ -266,13 +285,25 @@
 
         pltpu.make_async_copy(pair, pair, pair_send).wait()
 
-    def orthogonalize():
-        vecs[...] = p_full[...]
-        lanes = lax.broadcasted_iota(jnp.int32, t_vecs.shape, 1)
-        t_vecs[...] = (lanes == lax.broadcasted_iota(jnp.int32, t_vecs.shape, 0)).astype(F32)
-        for base in range(0, rank, 8):
-            band = pl.ds(base, 8)
-            above, left, t_left = p_full[band, :], vecs[band, :], t_vecs[band, :]
+    def orthogonalize(h):
+        first = h * band
+        if h == 0:
+            lanes = lax.broadcasted_iota(jnp.int32, t_vecs.shape, 1)
+            t_vecs[...] = (lanes == lax.broadcasted_iota(jnp.int32, t_vecs.shape, 0)).astype(F32)
+        vecs[rows_of(h), :] = p_full[rows_of(h), :]
+
+        def remove(unit, t_unit, rows):
+            for below in rows:
+                later = pl.ds(below, 8)
+                coef = jnp.sum(p_full[later, :] * unit, axis=1, keepdims=True)
+                vecs[later, :] = vecs[later, :] - coef * unit
+                t_vecs[later, :] = t_vecs[later, :] - coef * t_unit
+
+        for k in range(first):
+            remove(basis[k:k + 1, :], t_mat[k:k + 1, :], range(first, first + band, 8))
+        for base in range(first, first + band, 8):
+            eight = pl.ds(base, 8)
+            above, left, t_left = p_full[eight, :], vecs[eight, :], t_vecs[eight, :]
             done, t_done = [], []
             for k in range(8):
                 row = left[k:k + 1, :]
@@ -286,128 +317,124 @@
                 if k < 7:
                     left = left - (coef * inverse) * unit
                     t_left = t_left - (coef * inverse) * t_unit
-                for below in range(base + 8, rank, 8):
-                    later = pl.ds(below, 8)
-                    coef = jnp.sum(p_full[later, :] * unit, axis=1, keepdims=True)
-                    vecs[later, :] = vecs[later, :] - coef * unit
-                    t_vecs[later, :] = t_vecs[later, :] - coef * t_unit
-            basis[band, :] = jnp.concatenate(done, axis=0)
-            t_mat[band, :] = jnp.concatenate(t_done, axis=0)
-
-    def sum_p():
+                remove(unit, t_unit, range(base + 8, first + band, 8))
+            basis[eight, :] = jnp.concatenate(done, axis=0)
+            t_mat[eight, :] = jnp.concatenate(t_done, axis=0)
+
+    def sum_p(h):
         def body():
-            mine = window(p_cuts, p_part.shape, index_of(p_cuts, me))
-            drain(p_recv, p_rs_recv, count - 1)
-            p_full[mine] = p_part[mine] + jnp.sum(p_recv[...], axis=0)
+            mine = window(p_cuts, width, index_of(p_cuts, me), h)
+            drain(p_recv.at[h], p_rs_recv.at[h], count - 1)
+            p_full[mine] = p_part[mine] + jnp.sum(p_recv[h], axis=0)
 
             @pl.loop(1, count)
             def _(d):
                 pltpu.make_async_remote_copy(
                     src_ref=p_full.at[mine], dst_ref=p_full.at[mine],
-                    send_sem=p_ag_send, recv_sem=p_ag_recv.at[own_block],
+                    send_sem=p_ag_send.at[h], recv_sem=p_ag_recv.at[h],
                     device_id=(far_first(me, d, count),), device_id_type=MESH,
                 ).start()
 
-        either(p_cuts, me, body, lambda: None)
-
-    def await_block(index):
-        def own_or_other():
-            @pl.when(index == own_block)
-            def _():
-                drain(p_recv, p_ag_recv.at[index], sharers - 1)
-
-            @pl.when(index != own_block)
-            def _():
-                drain(p_recv, p_ag_recv.at[index], sharers)
-
-        either(p_cuts, me, own_or_other, lambda: drain(p_recv, p_ag_recv.at[index], sharers))
-
-    def send_group(group):
-        for j in range(members):
-            place = group * members + j
-            target = owner_of(q_cuts, place)
-
-            @pl.when(target != chip)
-            def _():
-                pltpu.make_async_remote_copy(
-                    src_ref=q_part.at[window(q_cuts, q_part.shape, place)],
-                    dst_ref=q_recv.at[lax.rem(target - chip + chips, chips) - 1],
-                    send_sem=q_rs_send, recv_sem=q_rs_recv,
-                    device_id=(2 * target + core,), device_id_type=MESH,
-                ).start()
-
-    def multiply():
-        @pl.loop(0, blocks)
-        def _(i):
-            await_block(near_first(own_block, i, blocks))
-
-        high, low = halves(p_full[...])
+        either(p_cuts, me, count, body, lambda: None)
+
+    def multiply(h):
+        either(
+            p_cuts, me, count,
+            lambda: drain(p_recv.at[h], p_ag_recv.at[h], p_owners - 1),
+            lambda: drain(p_recv.at[h], p_ag_recv.at[h], p_owners),
+        )
+        high, low = halves(p_full[rows_of(h), :])
         left = jnp.concatenate([high, low], axis=0)
-        b_split[...] = left
 
         @pl.loop(0, groups)
         def _(i):
             group = far_first(own_group, i + 1, groups)
             cols = local(group)
-            both = jnp.dot(b_split[...], m_hi[:, cols], preferred_element_type=F32)
-            both += jnp.dot(b_split[...], m_lo[:, cols], preferred_element_type=F32)
-            q_part[:, cols] = both[0:rank] + both[rank:2 * rank]
-            send_group(group)
-
-    def sum_q():
+            both = jnp.dot(left, m_hi[:, cols], preferred_element_type=F32)
+            both += jnp.dot(left, m_lo[:, cols], preferred_element_type=F32)
+            q_part[rows_of(h), cols] = both[0:band] + both[band:2 * band]
+
+            for j in range(members):
+                place = group * members + j
+                target = owner_of(q_cuts, place)
+
+                @pl.when(target != chip)
+                def _():
+                    pltpu.make_async_remote_copy(
+                        src_ref=q_part.at[window(q_cuts, half, place, h)],
+                        dst_ref=q_recv.at[h, lax.rem(target - chip + chips, chips) - 1],
+                        send_sem=q_rs_send.at[h], recv_sem=q_rs_recv.at[h],
+                        device_id=(2 * target + core,), device_id_type=MESH,
+                    ).start()
+
+    def sum_q(h):
         def body():
-            drain(q_recv, q_rs_recv, chips - 1)
+            drain(q_recv.at[h], q_rs_recv.at[h], chips - 1)
             index = index_of(q_cuts, chip)
-            total = q_part[window(q_cuts, q_part.shape, index)] + jnp.sum(q_recv[...], axis=0)
+            q_sum[rows_of(h), :] = q_part[window(q_cuts, half, index, h)] + jnp.sum(q_recv[h], axis=0)
+            done = (h + 1) * band
             rotated = jnp.dot(
-                t_mat[:, 0:rank], total, precision=lax.Precision.HIGHEST, preferred_element_type=F32
+                t_mat[rows_of(h), 0:done], q_sum[0:done, :],
+                precision=lax.Precision.HIGHEST, preferred_element_type=F32,
             )
-            mine = window(q_cuts, q_part.shape, index, own_base)
+            mine = window(q_cuts, half, index, h, own_base)
             q_full[mine] = rotated / count
 
             @pl.loop(1, chips)
             def _(d):
                 pltpu.make_async_remote_copy(
                     src_ref=q_full.at[mine], dst_ref=q_full.at[mine],
-                    send_sem=q_ag_send, recv_sem=q_ag_recv.at[own_group],
+                    send_sem=q_ag_send.at[h], recv_sem=q_ag_recv.at[h, own_group],
                     device_id=(2 * far_first(chip, d, chips) + core,), device_id_type=MESH,
                 ).start()
 
-        either(q_cuts, chip, body, lambda: None)
-
-    def await_group(group):
+        either(q_cuts, chip, chips, body, lambda: None)
+
+    def await_group(h, group):
+        def take(pieces):
+            drain(q_recv.at[h], q_ag_recv.at[h, group], pieces)
+
         def own_or_other():
-            @pl.when(group == own_group)
-            def _():
-                drain(q_recv, q_ag_recv.at[group], members - 1)
-
-            @pl.when(group != own_group)
-            def _():
-                drain(q_recv, q_ag_recv.at[group], members)
-
-        either(q_cuts, chip, own_or_other, lambda: drain(q_recv, q_ag_recv.at[group], members))
+            pl.when(group == own_group)(lambda: take(members - 1))
+            pl.when(group != own_group)(lambda: take(members))
+
+        either(q_cuts, chip, chips, own_or_other, lambda: take(members))
+
+    def drain_p(h):
+        drain_sends(p_cuts, me, count, p_recv.at[h], p_rs_send.at[h], p_ag_send.at[h])
+
+    def drain_q(h):
+        drain_sends(q_cuts, chip, chips, q_recv.at[h], q_rs_send.at[h], q_ag_send.at[h])
+
+    streams = range(STREAMS)
 
     @pl.loop(0, ITERS)
     def _(step):
-        sum_p()
+        for h in streams:
+            sum_p(h)
         pl.when(step == 0)(add_pair)
-        multiply()
-        orthogonalize()
-        sum_q()
-        drain_sends(p_cuts, me, count, p_recv, p_rs_send, p_ag_send)
+        for h in streams:
+            multiply(h)
+        for h in streams:
+            orthogonalize(h)
+            sum_q(h)
+        for h in streams:
+            drain_p(h)
 
         @pl.when(step < ITERS - 1)
         def _():
-            @pl.loop(0, groups - 1)
-            def _(i):
-                group = near_first(own_group, i, groups)
-                await_group(group)
-                absorb(group)
-
-            group = near_first(own_group, groups - 1, groups)
-            await_group(group)
-            absorb_last(group)
-            drain_sends(q_cuts, chip, chips, q_recv, q_rs_send, q_ag_send)
+            for h in streams:
+                @pl.loop(0, groups - 1)
+                def _(i):
+                    group = near_first(own_group, i, groups)
+                    await_group(h, group)
+                    absorb(h, group)
+
+                group = near_first(own_group, groups - 1, groups)
+                await_group(h, group)
+                absorb_last(h, group)
+            for h in streams:
+                drain_q(h)
 
     tall = basis[...].T
     high, low = halves(tall)
@@ -426,7 +453,8 @@
     @pl.loop(0, groups)
     def _(i):
         group = near_first(own_group, i, groups)
-        await_group(group)
+        for h in streams:
+            await_group(h, group)
         relay(own_base, group).start()
         cols = local(group)
         err_own[:, cols] = (merged[:, cols] - recon(b_tall, q_full, chunk(own_base, group))).astype(BF16)
@@ -435,7 +463,8 @@
     def _(i):
         relay(other_base, i).wait_recv()
 
-    drain_sends(q_cuts, chip, chips, q_recv, q_rs_send, q_ag_send)
+    for h in streams:
+        drain_q(h)
     pltpu.make_async_copy(q_part, q_part, relay_send).wait()
     q_out[...] = q_full[...]
 
@@ -503,8 +532,8 @@
     groups = half // CHUNK
     hbm_spec = pl.BlockSpec(memory_space=pltpu.HBM)
     vmem_spec = pl.BlockSpec(memory_space=pltpu.VMEM)
-    p_cuts, q_cuts = split_tiles(count, rank, width), split_columns(chips, half)
-    blocks = width // max(256, width // p_cuts[1])
+    band = rank // STREAMS
+    p_cuts, q_cuts = split_tiles(count, band, width), split_columns(chips, half)
     dma = pltpu.SemaphoreType.DMA
     parts = pl.pallas_call(
         functools.partial(kernel, count),
@@ -527,20 +556,21 @@
             pltpu.VMEM((width, half), BF16),
             pltpu.VMEM((rank, ff), F32),
             pltpu.VMEM((rank, half), F32),
-            pltpu.VMEM((chips - 1, rank // q_cuts[0], half // q_cuts[1]), F32),
-            pltpu.VMEM((2 * rank, width), BF16),
+            pltpu.VMEM((STREAMS, chips - 1, band, half // q_cuts[1]), F32),
+            pltpu.VMEM((rank, half // q_cuts[1]), F32),
             pltpu.VMEM((rank, width), F32),
             pltpu.VMEM((rank, width), F32),
-            pltpu.VMEM((count - 1, rank // p_cuts[0], width // p_cuts[1]), F32),
+            pltpu.VMEM((STREAMS, count - 1, band // p_cuts[0], width // p_cuts[1]), F32),
             pltpu.VMEM((rank, width), F32),
             pltpu.VMEM((rank, width), F32),
             pltpu.VMEM((rank, 128), F32),
             pltpu.VMEM((rank, 128), F32),
             pltpu.VMEM((width, 2 * rank), F32),
             pltpu.VMEM((tokens, 2 * rank), F32),
-            pltpu.VMEM((2 * rank, width), F32),
+            pltpu.VMEM((STREAMS, 2 * band, width), F32),
             dma, dma, dma((2 * groups,)), dma((2 * groups,)), dma, dma((groups,)), dma, dma((groups,)),
-            dma, dma, dma, dma((blocks,)), dma, dma, dma, dma((groups,)),
+            dma((STREAMS,)), dma((STREAMS,)), dma((STREAMS,)), dma((STREAMS,)),
+            dma((STREAMS,)), dma((STREAMS,)), dma((STREAMS,)), dma((STREAMS, groups)),
         ],
         compiler_params=pltpu.CompilerParams(
             collective_id=0, has_side_effects=True, vmem_limit_bytes=47 * 1024 * 1024

time: 98.5 us -> 88.6 us (0.90)
  Pallas kernels: 97.7 us -> 87.8 us
    pallas_call x1, Pallas kernels: 94 us -> 84.1 us  [shards(): pl.pallas_call(functools.partial(kernel, count), out_shape=(pltpu.VMEM((w...]
where the time goes in v3:
time: 88.6 us; the launch traced here: 88.5 us
  Pallas kernels  87.8 us (99%)
    pallas_call x1, Pallas kernels, shards(): pl.pallas_call(functools.partial(kernel, count), out_shape=(pltpu.VMEM((w...  84.1 us
    pallas_call x1, Pallas kernels, shards(): pl.pallas_call(finish, out_shape=(jax.ShapeDtypeStruct(error_in.shape, BF...  3.71 us

profile of v3, /device:TPU:0, one launch (start us, length us, event | category | flops | bytes accessed | tf_op | source)
XLA Modules:
  0.0 88.5 jit_solution(3457218580235476364)
XLA Ops:
  0.6 0.0 copy-start
  0.6 84.1 %shard_map.76 = (bf16[1024,2048]{1,0:T(8,128)(2,1)S(1)}, f32[1024,2048]{1,0:T(8,128)S(1)}, f32[32,4096]{1,0:T(8,128)S(1)}, bf16[1024,96]{1,0:T(8,128)(2,1)S(1)}) custom-call(bf16[512,1024]{1,0:T(8,128)(2,1)} %x_hbm.1, bf16[512,4096]{1,0:T(8,128)(2,1)} %dy_hbm.1, bf16[1,1024,4096]{2,1,0:T(8,128)(2,1)} %err_hbm.1, f32[32,4096]{1,0:T(8,128)} %start_hbm.1), custom_call_target="tpu_custom_call" | custom-call | tf_op jit(solution)/shard_map/pallas_call | solution.py:538
  84.8 0.0 copy-done
  84.8 3.7 %shard_map.77 = (bf16[1,1024,4096]{2,1,0:T(8,128)(2,1)}, f32[32,4096]{1,0:T(8,128)}, f32[1024,128]{1,0:T(8,128)}) custom-call(bf16[1024,2048]{1,0:T(8,128)(2,1)S(1)} %get-tuple-element.7.err_own, f32[1024,2048]{1,0:T(8,128)S(1)} %get-tuple-element.8.rest, f32[32,4096]{1,0:T(8,128)S(1)} %get-tuple-element.9.q_full, ...), custom_call_target="tpu_custom_call" | custom-call | tf_op jit(solution)/shard_map/pallas_call | solution.py:579
Async XLA Ops:
  0.6 84.1 %copy-start = (f32[1024,128]{1,0:T(8,128)S(1)}, f32[1024,128]{1,0:T(8,128)}, u32[]{:S(2)}) copy-start(f32[1024,128]{1,0:T(8,128)} %master_hbm.1) | copy-start | bytes 1572868

commit v4 on v3

--- a/solution.py
+++ b/solution.py
@@ -12,7 +12,7 @@
 MIDDLE = True
 AXIS = "rep"
 CHUNK = 512
-EARLY, LATE = 2, 3
+EARLY, LATE = 2, 4
 MESH = pl.DeviceIdType.MESH
 F32, BF16 = jnp.float32, jnp.bfloat16
 
@@ -34,16 +34,23 @@
     return high, (value - high.astype(F32)).astype(BF16)
 
 
+def far_part(own, step, parts):
+    down = parts - 1 - step
+    down = jnp.where(down <= own, down - 1, down)
+    up = jnp.where(step >= own, step + 1, step)
+    return jnp.where(step == parts - 1, own, jnp.where(2 * own < parts, down, up))
+
+
+def near_part(own, step, parts):
+    return far_part(own, parts - 1 - step, parts)
+
+
 def far_first(own, step, count):
-    if count & (count - 1) == 0:
-        return own ^ (count - step)
-    return lax.rem(own + step, count)
-
-
-def near_first(own, step, count):
-    if count & (count - 1) == 0:
-        return own ^ step
-    return lax.rem(own - step + count, count)
+    size = count // 4
+    if count % 4 or size & (size - 1):
+        return lax.rem(own + step, count)
+    plane = far_part(own // size, (step - 1) // size, 4)
+    return plane * size + (lax.rem(own, size) ^ (size - 1 - lax.rem(step - 1, size)))
 
 
 def kernel(
@@ -178,20 +185,30 @@
         high, low = halves(q_full[rows_of(h), chunk(own_base, group)])
         return jnp.concatenate([high, low], axis=0)
 
+    def turn():
+        @pl.loop(0, groups)
+        def _(i):
+            slot = pl.ds(pl.multiple_of(i * width, width), width)
+            err_v[0:cw, slot] = m_hi[:, local(i)].T
+            err_v[cw:2 * cw, slot] = m_lo[:, local(i)].T
+
+    def across(factor, group, shift, size):
+        slot = pl.ds(pl.multiple_of(group * width + shift, size), size)
+        return jnp.dot(factor, err_v[0:cw, slot], preferred_element_type=F32) + jnp.dot(
+            factor, err_v[cw:2 * cw, slot], preferred_element_type=F32
+        )
+
     def absorb(h, group):
-        factor = band_factor(h, group)
-        cols = local(group)
-        p_flat[h] += tall_dot(factor, m_hi[:, cols]) + tall_dot(factor, m_lo[:, cols])
+        p_flat[h] += across(band_factor(h, group), group, 0, width)
 
     def absorb_last(h, group):
         factor = band_factor(h, group)
-        cols = local(group)
 
         @pl.loop(0, blocks)
         def _(i):
-            index = far_first(own_block, i + 1, blocks)
+            index = far_part(own_block, i, blocks)
             rows = block_of(index)
-            flat = p_flat[h, :, rows] + tall_dot(factor, m_hi[rows, cols]) + tall_dot(factor, m_lo[rows, cols])
+            flat = p_flat[h, :, rows] + across(factor, group, index * block, block)
             p_part[rows_of(h), rows] = flat[0:band] + flat[band:2 * band]
             send_block(h, index)
 
@@ -245,7 +262,7 @@
 
     @pl.loop(0, blocks)
     def _(i):
-        index = far_first(own_block, i + 1, blocks)
+        index = far_part(own_block, i, blocks)
         cols = block_of(index)
         flat = p_tall[cols, :].T + jnp.dot(u_split, x_v[:, cols], preferred_element_type=F32)
         p_part[:, cols] = flat[0:rank] + flat[rank:2 * rank]
@@ -255,7 +272,7 @@
 
         @pl.loop(0, blocks)
         def _(i):
-            send_block(h, far_first(own_block, i + 1, blocks))
+            send_block(h, far_part(own_block, i, blocks))
 
     p_flat[...] = jnp.zeros_like(p_flat)
 
@@ -348,7 +365,7 @@
 
         @pl.loop(0, groups)
         def _(i):
-            group = far_first(own_group, i + 1, groups)
+            group = far_part(own_group, i, groups)
             cols = local(group)
             both = jnp.dot(left, m_hi[:, cols], preferred_element_type=F32)
             both += jnp.dot(left, m_lo[:, cols], preferred_element_type=F32)
@@ -418,6 +435,7 @@
         for h in streams:
             orthogonalize(h)
             sum_q(h)
+        pl.when(step == 0)(turn)
         for h in streams:
             drain_p(h)
 
@@ -426,11 +444,11 @@
             for h in streams:
                 @pl.loop(0, groups - 1)
                 def _(i):
-                    group = near_first(own_group, i, groups)
+                    group = near_part(own_group, i, groups)
                     await_group(h, group)
                     absorb(h, group)
 
-                group = near_first(own_group, groups - 1, groups)
+                group = near_part(own_group, groups - 1, groups)
                 await_group(h, group)
                 absorb_last(h, group)
             for h in streams:
@@ -452,7 +470,7 @@
 
     @pl.loop(0, groups)
     def _(i):
-        group = near_first(own_group, i, groups)
+        group = near_part(own_group, i, groups)
         for h in streams:
             await_group(h, group)
         relay(own_base, group).start()
@@ -530,6 +548,7 @@
     rank = q_start.shape[0]
     chips, half = count // 2, ff // 2
     groups = half // CHUNK
+    assert 2 * CHUNK <= width and groups * width <= ff
     hbm_spec = pl.BlockSpec(memory_space=pltpu.HBM)
     vmem_spec = pl.BlockSpec(memory_space=pltpu.VMEM)
     band = rank // STREAMS

time: 88.6 us -> 87.6 us (0.989)
  Pallas kernels: 87.8 us -> 86.8 us
    pallas_call x1, Pallas kernels: 84.1 us -> 83.1 us  [shards(): pl.pallas_call(functools.partial(kernel, count), out_shape=(pltpu.VMEM((w...]
where the time goes in v4:
time: 87.6 us; the launch traced here: 87.4 us
  Pallas kernels  86.8 us (99%)
    pallas_call x1, Pallas kernels, shards(): pl.pallas_call(functools.partial(kernel, count), out_shape=(pltpu.VMEM((w...  83.1 us
    pallas_call x1, Pallas kernels, shards(): pl.pallas_call(finish, out_shape=(jax.ShapeDtypeStruct(error_in.shape, BF...  3.71 us

profile of v4, /device:TPU:0, one launch (start us, length us, event | category | flops | bytes accessed | tf_op | source)
XLA Modules:
  0.0 87.4 jit_solution(4438238573709279846)
XLA Ops:
  0.6 0.0 copy-start
  0.6 83.1 %shard_map.76 = (bf16[1024,2048]{1,0:T(8,128)(2,1)S(1)}, f32[1024,2048]{1,0:T(8,128)S(1)}, f32[32,4096]{1,0:T(8,128)S(1)}, bf16[1024,96]{1,0:T(8,128)(2,1)S(1)}) custom-call(bf16[512,1024]{1,0:T(8,128)(2,1)} %x_hbm.1, bf16[512,4096]{1,0:T(8,128)(2,1)} %dy_hbm.1, bf16[1,1024,4096]{2,1,0:T(8,128)(2,1)} %err_hbm.1, f32[32,4096]{1,0:T(8,128)} %start_hbm.1), custom_call_target="tpu_custom_call" | custom-call | tf_op jit(solution)/shard_map/pallas_call | solution.py:557
  83.7 0.0 copy-done
  83.7 3.7 %shard_map.77 = (bf16[1,1024,4096]{2,1,0:T(8,128)(2,1)}, f32[32,4096]{1,0:T(8,128)}, f32[1024,128]{1,0:T(8,128)}) custom-call(bf16[1024,2048]{1,0:T(8,128)(2,1)S(1)} %get-tuple-element.7.err_own, f32[1024,2048]{1,0:T(8,128)S(1)} %get-tuple-element.8.rest, f32[32,4096]{1,0:T(8,128)S(1)} %get-tuple-element.9.q_full, ...), custom_call_target="tpu_custom_call" | custom-call | tf_op jit(solution)/shard_map/pallas_call | solution.py:598
Async XLA Ops:
  0.6 83.1 %copy-start = (f32[1024,128]{1,0:T(8,128)S(1)}, f32[1024,128]{1,0:T(8,128)}, u32[]{:S(2)}) copy-start(f32[1024,128]{1,0:T(8,128)} %master_hbm.1) | copy-start | bytes 1572868
